TPU v7x, 32 devices: a whole 2x2x4 slice. The times are simulated.
32 devices in a mesh: dp: 2 (over core), sx: 4 (over y, x), sy: 4 (over z).
Axes of the slice: x: 2, y: 2, z: 4, core: 2. Of those that a mesh axis runs over, the one named last changes fastest.
Arguments:
- volume: bfloat16 [2, 32, 32, 32, 128], P('dp', None, 'sx', 'sy'), may hold values from -6 to 6
- conv_one: bfloat16 [2, 32, 32, 32, 128], P('dp', None, 'sx', 'sy'), may hold values from -300 to 300
- conv_two: bfloat16 [2, 32, 32, 32, 128], P('dp', None, 'sx', 'sy'), may hold values from -300 to 300
- upper_grad: bfloat16 [2, 32, 32, 32, 128], P('dp', None, 'sx', 'sy'), may hold values from -36 to 36
- weight_one: bfloat16 [3, 3, 3, 32, 32], replicated, may hold values from -0.21875 to 0.21875
- weight_two: bfloat16 [3, 3, 3, 32, 32], replicated, may hold values from -0.21875 to 0.21875
- gain_one: float32 [32], replicated, may hold values from 0.1 to 1.9
- bias_one: float32 [32], replicated, may hold values from -1 to 1
- gain_two: float32 [32], replicated, may hold values from 0.1 to 1.9
- bias_two: float32 [32], replicated, may hold values from -1 to 1
Outputs:
- input_grad: bfloat16 [2, 32, 32, 32, 128], P('dp', None, 'sx', 'sy')
- weight_one_grad: float32 [3, 3, 3, 32, 32], replicated
- weight_two_grad: float32 [3, 3, 3, 32, 32], replicated
- gain_one_grad: float32 [32], replicated
- bias_one_grad: float32 [32], replicated
- gain_two_grad: float32 [32], replicated
- bias_two_grad: float32 [32], replicated
All inputs are finite; a program needn't handle non-finite values.
Results may differ from a plain program's by a relative error of at most 0.014.
Values may be sent and summed in bfloat16 or wider, within the bound.
A program may use at most 64 MiB of HBM per device.

v0:
```python
import math

import jax
import jax.numpy as jnp
from jax import lax
from jax.sharding import PartitionSpec as P

epsilon = 1e-05


def extended_2(array, sides, width):
    for axis, dim in sides:
        size, length = (lax.axis_size(axis), array.shape[dim])
        up = [(i, (i + 1) % size) for i in range(size - 1)]
        down = [(j, i) for i, j in up]
        last = lax.slice_in_dim(array, length - width, length, axis=dim)
        first = lax.slice_in_dim(array, 0, width, axis=dim)
        before = lax.ppermute(last, axis, up)
        after = lax.ppermute(first, axis, down)
        array = jnp.concatenate([before, array, after], axis=dim)
    return array


def channel(vector):
    return vector[None, :, None, None, None]


def local_sum(values):
    return jnp.sum(values, axis=(0, 2, 3, 4))


def extended(values):
    widened = extended_2(values, (("sx", 2), ("sy", 3)), 1)
    return jnp.pad(widened, ((0, 0), (0, 0), (0, 0), (0, 0), (1, 1)))


def back_project(padded, shape, weight):
    extent_x, extent_y, extent_z = (shape[2], shape[3], shape[4])
    total = jnp.zeros(shape, jnp.float32)
    for shift_x in range(3):
        for shift_y in range(3):
            for shift_z in range(3):
                piece = padded[
                    :,
                    :,
                    2 - shift_x : 2 - shift_x + extent_x,
                    2 - shift_y : 2 - shift_y + extent_y,
                    2 - shift_z : 2 - shift_z + extent_z,
                ]
                total = total + jnp.einsum(
                    "co,boxyz->bcxyz",
                    weight[shift_x, shift_y, shift_z],
                    piece,
                    preferred_element_type=jnp.float32,
                )
    return total


def filter_terms(values, gradient):
    padded = extended(values)
    extent_x, extent_y, extent_z = (gradient.shape[2], gradient.shape[3], gradient.shape[4])
    blocks = []
    for shift_x in range(3):
        for shift_y in range(3):
            for shift_z in range(3):
                piece = padded[
                    :,
                    :,
                    shift_x : shift_x + extent_x,
                    shift_y : shift_y + extent_y,
                    shift_z : shift_z + extent_z,
                ]
                blocks.append(
                    jnp.einsum(
                        "bcxyz,boxyz->co", piece, gradient, preferred_element_type=jnp.float32
                    )
                )
    return jnp.stack(blocks).reshape(3, 3, 3, values.shape[1], gradient.shape[1])


def filter_gradient(values, gradient):
    return filter_terms(values, gradient)


def silu_slope(inputs):
    logistic = jax.nn.sigmoid(inputs)
    return logistic * (1.0 + inputs * (1.0 - logistic))


def normalized(saved, total, squares, gain, offset, cell_count):
    average = total / cell_count
    spread = squares / cell_count - average * average
    inv_std = lax.rsqrt(spread + epsilon)
    centered = (saved.astype(jnp.float32) - channel(average)) * channel(inv_std)
    shifted = channel(gain) * centered + channel(offset)
    return (centered, shifted, inv_std)


def norm_backward(upstream, centered, shifted, inv_std, gain, cell_count):
    slope_grad = upstream * silu_slope(shifted)
    bias_total, gain_total = lax.psum(
        (local_sum(slope_grad), local_sum(slope_grad * centered)), ("dp", "sx", "sy")
    )
    pre_grad = channel(gain * inv_std) * (
        slope_grad - channel(bias_total / cell_count) - centered * channel(gain_total / cell_count)
    )
    return (pre_grad.astype(jnp.bfloat16), gain_total, bias_total)


def reduce_filters(filters):
    return lax.psum(tuple(filters), ("dp", "sx", "sy"))


def per_device(
    volume,
    conv_one,
    conv_two,
    upper_grad,
    weight_one,
    weight_two,
    gain_one,
    bias_one,
    gain_two,
    bias_two,
):
    cell_count = float(
        volume.shape[0]
        * lax.axis_size("dp")
        * volume.shape[2]
        * lax.axis_size("sx")
        * volume.shape[3]
        * lax.axis_size("sy")
        * volume.shape[4]
    )
    saved_one = conv_one.astype(jnp.float32)
    saved_two = conv_two.astype(jnp.float32)
    moments = lax.psum(
        (
            local_sum(saved_one),
            local_sum(saved_one * saved_one),
            local_sum(saved_two),
            local_sum(saved_two * saved_two),
        ),
        ("dp", "sx", "sy"),
    )
    cent_one, shift_one, inv_one = normalized(
        conv_one, moments[0], moments[1], gain_one, bias_one, cell_count
    )
    activation = jax.nn.silu(shift_one).astype(jnp.bfloat16)
    cent_two, shift_two, inv_two = normalized(
        conv_two, moments[2], moments[3], gain_two, bias_two, cell_count
    )
    grad_two, gain_two_total, bias_two_total = norm_backward(
        upper_grad.astype(jnp.float32), cent_two, shift_two, inv_two, gain_two, cell_count
    )
    rim_two = extended(grad_two)
    upstream = back_project(rim_two, grad_two.shape, weight_two)
    filter_two = filter_gradient(activation, grad_two)
    filter_two = reduce_filters([filter_two])[0]
    grad_one, gain_one_total, bias_one_total = norm_backward(
        upstream, cent_one, shift_one, inv_one, gain_one, cell_count
    )
    rim_one = extended(grad_one)
    input_grad = back_project(rim_one, grad_one.shape, weight_one).astype(jnp.bfloat16)
    filter_one = filter_gradient(volume, grad_one)
    filter_one = reduce_filters([filter_one])[0]
    factor = 1.0 / math.sqrt(cell_count)
    return (
        input_grad,
        filter_one * factor,
        filter_two * factor,
        gain_one_total * factor,
        bias_one_total * factor,
        gain_two_total * factor,
        bias_two_total * factor,
    )


def solution(mesh):
    return jax.shard_map(
        per_device,
        mesh=mesh,
        in_specs=(
            P("dp", None, "sx", "sy", None),
            P("dp", None, "sx", "sy", None),
            P("dp", None, "sx", "sy", None),
            P("dp", None, "sx", "sy", None),
            P(),
            P(),
            P(),
            P(),
            P(),
            P(),
        ),
        out_specs=(P("dp", None, "sx", "sy", None), P(), P(), P(), P(), P(), P()),
        check_vma=False,
    )
```

profile of v0, /device:TPU:0, one launch (start us, length us, event | category | flops | bytes accessed | tf_op | source)
XLA Modules:
  0.0 397.5 jit_solution(16901678759860612227)
XLA Ops:
  10.1 42.0 %all-reduce.6 = (f32[32]{0:T(128)S(1)}, f32[32]{0:T(128)S(1)}) all-reduce(f32[32]{0:T(128)S(1)} %get-tuple-element.21, f32[32]{0:T(128)S(1)} %get-tuple-element.20), channel_id=1, replica_groups=mesh['dp'=2,'sx'=4,'sy'=4] {'dp','sx','sy'}, use_global_device_ids=true, to_apply=%region_5.0 | all-reduce | flops 64 | bytes 512 | tf_op jit(solution)/shard_map/psum | solution.py:137
  52.8 2.3 fusion.394
  55.1 40.1 %all-reduce.5 = (f32[32]{0:T(128)S(1)}, f32[32]{0:T(128)S(1)}, f32[32]{0:T(128)S(1)}, f32[32]{0:T(128)S(1)}) all-reduce(f32[32]{0:T(128)S(1)} %get-tuple-element.17, f32[32]{0:T(128)S(1)} %get-tuple-element.16, f32[32]{0:T(128)S(1)} %get-tuple-element.19, ...), channel_id=1, replica_groups=mesh['dp'=2,'sx'=4,'sy'=4] {'dp','sx','sy'}, use_global_device_ids=true, to_apply=%region_11.12 | all-reduce | flops 128 | bytes 1024 | tf_op jit(solution)/shard_map/psum | solution.py:101
  96.3 4.2 %collective-permute-start = (bf16[1,32,1,8,128]{4,1,3,2,0:T(8,128)(2,1)S(1)}, bf16[1,32,1,8,128]{4,1,3,2,0:T(8,128)(2,1)S(1)}, u32[]{:S(2)}, u32[]{:S(2)}) collective-permute-start(bf16[1,32,1,8,128]{4,1,3,2,0:T(8,128)(2,1)S(1)} %get-tuple-element.56), channel_id=1, source_target_pairs={{0,4},{4,8},{8,12},{1,5},{5,9},{9,13},{2,6},{6,10},{10,14},{3,7},{... | collective-permute-start | bytes 196616 | tf_op jit(solution)/shard_map/ppermute | solution.py:18
  102.1 4.5 %collective-permute-start.8 = (bf16[1,32,1,8,128]{4,1,3,2,0:T(8,128)(2,1)S(1)}, bf16[1,32,1,8,128]{4,1,3,2,0:T(8,128)(2,1)S(1)}, u32[]{:S(2)}, u32[]{:S(2)}) collective-permute-start(bf16[1,32,1,8,128]{4,1,3,2,0:T(8,128)(2,1)S(1)} %get-tuple-element.53), channel_id=1, source_target_pairs={{0,4},{4,8},{8,12},{1,5},{5,9},{9,13},{2,6},{6,10},{10,14},{3,7},{... | collective-permute-start | bytes 196616 | tf_op jit(solution)/shard_map/ppermute | solution.py:18
  108.4 2.4 collective-permute-start.2
  114.0 3.8 collective-permute-start.10
  117.8 1.6 collective-permute-start.11
  120.7 1.5 fusion.10
  130.2 2.6 fusion.393
  132.8 5.0 %collective-permute-start.12 = (bf16[1,32,1,8,128]{4,1,3,2,0:T(8,128)(2,1)S(1)}, bf16[1,32,1,8,128]{4,1,3,2,0:T(8,128)(2,1)S(1)}, u32[]{:S(2)}, u32[]{:S(2)}) collective-permute-start(bf16[1,32,1,8,128]{4,1,3,2,0:T(8,128)(2,1)S(1)} %get-tuple-element.50), channel_id=1, source_target_pairs={{0,4},{4,8},{8,12},{1,5},{5,9},{9,13},{2,6},{6,10},{10,14},{3,7},{... | collective-permute-start | bytes 196616 | tf_op jit(solution)/shard_map/ppermute | solution.py:18
  139.1 43.9 %all-reduce.4 = (f32[32]{0:T(128)S(1)}, f32[32]{0:T(128)S(1)}) all-reduce(f32[32]{0:T(128)S(1)} %get-tuple-element.15, f32[32]{0:T(128)S(1)} %get-tuple-element.14), channel_id=1, replica_groups=mesh['dp'=2,'sx'=4,'sy'=4] {'dp','sx','sy'}, use_global_device_ids=true, to_apply=%region_15.16 | all-reduce | flops 64 | bytes 512 | tf_op jit(solution)/shard_map/psum | solution.py:101
  184.1 1.7 fusion.125
  195.9 4.8 %collective-permute-start.4 = (bf16[1,32,1,8,128]{4,1,3,2,0:T(8,128)(2,1)S(1)}, bf16[1,32,1,8,128]{4,1,3,2,0:T(8,128)(2,1)S(1)}, u32[]{:S(2)}, u32[]{:S(2)}) collective-permute-start(bf16[1,32,1,8,128]{4,1,3,2,0:T(8,128)(2,1)S(1)} %get-tuple-element.54), channel_id=1, source_target_pairs={{0,4},{4,8},{8,12},{1,5},{5,9},{9,13},{2,6},{6,10},{10,14},{3,7},{... | collective-permute-start | bytes 196616 | tf_op jit(solution)/shard_map/ppermute | solution.py:18
  202.7 3.3 collective-permute-start.14
  207.3 4.6 %collective-permute-start.6 = (bf16[1,32,10,1,128]{4,1,3,2,0:T(8,128)(2,1)S(1)}, bf16[1,32,10,1,128]{4,1,3,2,0:T(8,128)(2,1)S(1)}, u32[]{:S(2)}, u32[]{:S(2)}) collective-permute-start(bf16[1,32,10,1,128]{4,1,3,2,0:T(8,128)(2,1)S(1)} %get-tuple-element.43), channel_id=1, source_target_pairs={{0,1},{1,2},{2,3},{4,5},{5,6},{6,7},{8,9},{9,10},{10,11},{12,13},{... | collective-permute-start | bytes 245768 | tf_op jit(solution)/shard_map/ppermute | solution.py:18
  215.9 2.3 collective-permute-done.7
  220.9 1.5 select_maximum_fusion.6
  246.1 1.7 select_maximum_fusion
  257.2 4.5 %fusion.25 = f32[8,8,128,32]{2,3,1,0:T(8,128)S(1)} fusion(f32[8,8,128,32]{2,3,1,0:T(8,128)} %fusion.179, f32[8,8,128,32]{2,3,1,0:T(8,128)} %fusion.180, f32[8,8,128,32]{2,3,1,0:T(8,128)} %fusion.181, f32[8,8,128,32]{2,3,1,0:T(8,128)} %fusion.182, f32[8,8,128,32]{2,3,1,0:T(8,128)} %fusion.183, f32[8,8,128,32]{2,3,1,0:T(8,128)S(1)} %copy-done.3, ...), kind=kOutput, calls=%fused_computation.69 | convolution fusion | flops 19398656 | bytes 12066816 | tf_op jit(solution)/shard_map/co,boxyz->bcxyz/dot_general | solution.py:50
  263.0 1.5 fusion.51
  268.2 118.6 %all-reduce.10.cloned.1.call-done = (f32[3,3,3,32,32]{4,3,2,1,0:T(8,128)}, f32[3,3,3,32,32]{4,3,2,1,0:T(8,128)}) async-done(((f32[3,3,3,32,32]{4,3,2,1,0:T(8,128)}, f32[3,3,3,32,32]{4,3,2,1,0:T(8,128)}), (f32[3,3,3,32,32]{4,3,2,1,0:T(8,128)}, f32[3,3,3,32,32]{4,3,2,1,0:T(8,128)})) %all-reduce.10.cloned.1.call-update) | async-done | bytes 221200 | tf_op jit(solution)/shard_map/psum | solution.py:111
  386.8 1.8 broadcast_multiply_fusion
  388.6 1.8 broadcast_multiply_fusion.1
  (216 shorter events, 80.1 us)
Async XLA Ops:
  7.2 88.6 %copy-start = (bf16[1,32,8,8,128]{4,3,2,1,0:T(8,128)(2,1)S(1)}, bf16[1,32,8,8,128]{4,3,2,1,0:T(8,128)(2,1)}, u32[]{:S(2)}) copy-start(bf16[1,32,8,8,128]{4,3,2,1,0:T(8,128)(2,1)} %param.12) | copy-start | bytes 1572868
  7.2 379.6 %all-reduce.10.cloned.1.call-start = ((), (), s32[]{:S(2)}) async-start(), calls=%async_computation | async-start | bytes 1769472 | tf_op jit(solution)/shard_map/psum | solution.py:111
  55.1 46.6 %copy-start.16 = (bf16[1,32,8,8,128]{4,3,2,1,0:T(8,128)(2,1)S(1)}, bf16[1,32,8,8,128]{4,3,2,1,0:T(8,128)(2,1)}, u32[]{:S(2)}) copy-start(bf16[1,32,8,8,128]{4,3,2,1,0:T(8,128)(2,1)} %param.10) | copy-start | bytes 1572868
  95.8 12.2 %copy-start.23 = (bf16[3,3,3,32,32]{4,3,2,1,0:T(8,128)(2,1)S(1)}, bf16[3,3,3,32,32]{4,3,2,1,0:T(8,128)(2,1)}, u32[]{:S(2)}) copy-start(bf16[3,3,3,32,32]{4,3,2,1,0:T(8,128)(2,1)} %param.15) | copy-start | bytes 165892
  96.2 12.1 %copy-start.29 = (f32[32]{0:T(128)S(1)}, f32[32]{0:T(128)}, u32[]{:S(2)}) copy-start(f32[32]{0:T(128)} %param.16) | copy-start | bytes 388
  96.3 12.1 %collective-permute-start = (bf16[1,32,1,8,128]{4,1,3,2,0:T(8,128)(2,1)S(1)}, bf16[1,32,1,8,128]{4,1,3,2,0:T(8,128)(2,1)S(1)}, u32[]{:S(2)}, u32[]{:S(2)}) collective-permute-start(bf16[1,32,1,8,128]{4,1,3,2,0:T(8,128)(2,1)S(1)} %get-tuple-element.56), channel_id=1, source_target_pairs={{0,4},{4,8},{8,12},{1,5},{5,9},{9,13},{2,6},{6,10},{10,14},{3,7},{... | collective-permute-start | bytes 196616 | tf_op jit(solution)/shard_map/ppermute | solution.py:18
  100.4 7.9 %collective-permute-start.1 = (bf16[1,32,1,8,128]{4,1,3,2,0:T(8,128)(2,1)S(1)}, bf16[1,32,1,8,128]{4,1,3,2,0:T(8,128)(2,1)S(1)}, u32[]{:S(2)}, u32[]{:S(2)}) collective-permute-start(bf16[1,32,1,8,128]{4,1,3,2,0:T(8,128)(2,1)S(1)} %get-tuple-element.57), channel_id=1, source_target_pairs={{4,0},{8,4},{12,8},{5,1},{9,5},{13,9},{6,2},{10,6},{14,10},{7,3},{... | collective-permute-start | bytes 196616 | tf_op jit(solution)/shard_map/ppermute | solution.py:19
  102.1 10.4 %copy-start.19 = (bf16[1,32,8,8,128]{4,1,3,2,0:T(8,128)(2,1)}, bf16[1,32,8,8,128]{4,1,3,2,0:T(8,128)(2,1)S(1)}, u32[]{:S(2)}) copy-start(bf16[1,32,8,8,128]{4,1,3,2,0:T(8,128)(2,1)S(1)} %copy.20) | copy-start | bytes 1572868
  102.1 9.9 %collective-permute-start.8 = (bf16[1,32,1,8,128]{4,1,3,2,0:T(8,128)(2,1)S(1)}, bf16[1,32,1,8,128]{4,1,3,2,0:T(8,128)(2,1)S(1)}, u32[]{:S(2)}, u32[]{:S(2)}) collective-permute-start(bf16[1,32,1,8,128]{4,1,3,2,0:T(8,128)(2,1)S(1)} %get-tuple-element.53), channel_id=1, source_target_pairs={{0,4},{4,8},{8,12},{1,5},{5,9},{9,13},{2,6},{6,10},{10,14},{3,7},{... | collective-permute-start | bytes 196616 | tf_op jit(solution)/shard_map/ppermute | solution.py:18
  106.7 6.5 %collective-permute-start.9 = (bf16[1,32,1,8,128]{4,1,3,2,0:T(8,128)(2,1)S(1)}, bf16[1,32,1,8,128]{4,1,3,2,0:T(8,128)(2,1)S(1)}, u32[]{:S(2)}, u32[]{:S(2)}) collective-permute-start(bf16[1,32,1,8,128]{4,1,3,2,0:T(8,128)(2,1)S(1)} %get-tuple-element.52), channel_id=1, source_target_pairs={{4,0},{8,4},{12,8},{5,1},{9,5},{13,9},{6,2},{10,6},{14,10},{7,3},{... | collective-permute-start | bytes 196616 | tf_op jit(solution)/shard_map/ppermute | solution.py:19
  108.4 11.6 %collective-permute-start.2 = (bf16[1,32,10,1,128]{4,1,3,2,0:T(8,128)(2,1)S(1)}, bf16[1,32,10,1,128]{4,1,3,2,0:T(8,128)(2,1)S(1)}, u32[]{:S(2)}, u32[]{:S(2)}) collective-permute-start(bf16[1,32,10,1,128]{4,1,3,2,0:T(8,128)(2,1)S(1)} %get-tuple-element.47), channel_id=1, source_target_pairs={{0,1},{1,2},{2,3},{4,5},{5,6},{6,7},{8,9},{9,10},{10,11},{12,13},{... | collective-permute-start | bytes 245768 | tf_op jit(solution)/shard_map/ppermute | solution.py:18
  110.8 9.2 %collective-permute-start.3 = (bf16[1,32,10,1,128]{4,1,3,2,0:T(8,128)(2,1)S(1)}, bf16[1,32,10,1,128]{4,1,3,2,0:T(8,128)(2,1)S(1)}, u32[]{:S(2)}, u32[]{:S(2)}) collective-permute-start(bf16[1,32,10,1,128]{4,1,3,2,0:T(8,128)(2,1)S(1)} %get-tuple-element.48), channel_id=1, source_target_pairs={{1,0},{2,1},{3,2},{5,4},{6,5},{7,6},{9,8},{10,9},{11,10},{13,12},{... | collective-permute-start | bytes 245768 | tf_op jit(solution)/shard_map/ppermute | solution.py:19
  114.0 71.8 %collective-permute-start.10 = (bf16[1,32,10,1,128]{4,1,3,2,0:T(8,128)(2,1)}, bf16[1,32,10,1,128]{4,1,3,2,0:T(8,128)(2,1)S(1)}, u32[]{:S(2)}, u32[]{:S(2)}) collective-permute-start(bf16[1,32,10,1,128]{4,1,3,2,0:T(8,128)(2,1)} %get-tuple-element.39), channel_id=1, source_target_pairs={{0,1},{1,2},{2,3},{4,5},{5,6},{6,7},{8,9},{9,10},{10,11},{12,13},{... | collective-permute-start | bytes 245768 | tf_op jit(solution)/shard_map/ppermute | solution.py:18
  117.8 68.0 %collective-permute-start.11 = (bf16[1,32,10,1,128]{4,1,3,2,0:T(8,128)(2,1)}, bf16[1,32,10,1,128]{4,1,3,2,0:T(8,128)(2,1)S(1)}, u32[]{:S(2)}, u32[]{:S(2)}) collective-permute-start(bf16[1,32,10,1,128]{4,1,3,2,0:T(8,128)(2,1)} %get-tuple-element.40), channel_id=1, source_target_pairs={{1,0},{2,1},{3,2},{5,4},{6,5},{7,6},{9,8},{10,9},{11,10},{13,12},{... | collective-permute-start | bytes 245768 | tf_op jit(solution)/shard_map/ppermute | solution.py:19
  132.8 53.0 %copy-start.18 = (bf16[1,32,10,8,128]{4,1,3,2,0:T(8,128)(2,1)S(1)}, bf16[1,32,10,8,128]{4,1,3,2,0:T(8,128)(2,1)}, u32[]{:S(2)}) copy-start(bf16[1,32,10,8,128]{4,1,3,2,0:T(8,128)(2,1)} %copy-done.17) | copy-start | bytes 1966084
  132.8 69.8 %collective-permute-start.12 = (bf16[1,32,1,8,128]{4,1,3,2,0:T(8,128)(2,1)S(1)}, bf16[1,32,1,8,128]{4,1,3,2,0:T(8,128)(2,1)S(1)}, u32[]{:S(2)}, u32[]{:S(2)}) collective-permute-start(bf16[1,32,1,8,128]{4,1,3,2,0:T(8,128)(2,1)S(1)} %get-tuple-element.50), channel_id=1, source_target_pairs={{0,4},{4,8},{8,12},{1,5},{5,9},{9,13},{2,6},{6,10},{10,14},{3,7},{... | collective-permute-start | bytes 196616 | tf_op jit(solution)/shard_map/ppermute | solution.py:18
  137.8 64.8 %collective-permute-start.13 = (bf16[1,32,1,8,128]{4,1,3,2,0:T(8,128)(2,1)S(1)}, bf16[1,32,1,8,128]{4,1,3,2,0:T(8,128)(2,1)S(1)}, u32[]{:S(2)}, u32[]{:S(2)}) collective-permute-start(bf16[1,32,1,8,128]{4,1,3,2,0:T(8,128)(2,1)S(1)} %get-tuple-element.51), channel_id=1, source_target_pairs={{4,0},{8,4},{12,8},{5,1},{9,5},{13,9},{6,2},{10,6},{14,10},{7,3},{... | collective-permute-start | bytes 196616 | tf_op jit(solution)/shard_map/ppermute | solution.py:19
  194.6 12.7 %collective-permute-start.5 = (bf16[1,32,1,8,128]{4,1,3,2,0:T(8,128)(2,1)S(1)}, bf16[1,32,1,8,128]{4,1,3,2,0:T(8,128)(2,1)S(1)}, u32[]{:S(2)}, u32[]{:S(2)}) collective-permute-start(bf16[1,32,1,8,128]{4,1,3,2,0:T(8,128)(2,1)S(1)} %get-tuple-element.55), channel_id=1, source_target_pairs={{4,0},{8,4},{12,8},{5,1},{9,5},{13,9},{6,2},{10,6},{14,10},{7,3},{... | collective-permute-start | bytes 196616 | tf_op jit(solution)/shard_map/ppermute | solution.py:19
  195.9 11.4 %collective-permute-start.4 = (bf16[1,32,1,8,128]{4,1,3,2,0:T(8,128)(2,1)S(1)}, bf16[1,32,1,8,128]{4,1,3,2,0:T(8,128)(2,1)S(1)}, u32[]{:S(2)}, u32[]{:S(2)}) collective-permute-start(bf16[1,32,1,8,128]{4,1,3,2,0:T(8,128)(2,1)S(1)} %get-tuple-element.54), channel_id=1, source_target_pairs={{0,4},{4,8},{8,12},{1,5},{5,9},{9,13},{2,6},{6,10},{10,14},{3,7},{... | collective-permute-start | bytes 196616 | tf_op jit(solution)/shard_map/ppermute | solution.py:18
  202.6 12.0 %copy-start.22 = (f32[27,32,32]{2,1,0:T(8,128)}, f32[27,32,32]{2,1,0:T(8,128)S(1)}, u32[]{:S(2)}) copy-start(f32[27,32,32]{2,1,0:T(8,128)S(1)} %fusion.80) | copy-start | bytes 331780
  202.7 43.4 %collective-permute-start.14 = (bf16[1,32,10,1,128]{4,1,3,2,0:T(8,128)(2,1)S(1)}, bf16[1,32,10,1,128]{4,1,3,2,0:T(8,128)(2,1)S(1)}, u32[]{:S(2)}, u32[]{:S(2)}) collective-permute-start(bf16[1,32,10,1,128]{4,1,3,2,0:T(8,128)(2,1)S(1)} %get-tuple-element.37), channel_id=1, source_target_pairs={{0,1},{1,2},{2,3},{4,5},{5,6},{6,7},{8,9},{9,10},{10,11},{12,13},{... | collective-permute-start | bytes 245768 | tf_op jit(solution)/shard_map/ppermute | solution.py:18
  206.0 40.1 %collective-permute-start.15 = (bf16[1,32,10,1,128]{4,1,3,2,0:T(8,128)(2,1)S(1)}, bf16[1,32,10,1,128]{4,1,3,2,0:T(8,128)(2,1)S(1)}, u32[]{:S(2)}, u32[]{:S(2)}) collective-permute-start(bf16[1,32,10,1,128]{4,1,3,2,0:T(8,128)(2,1)S(1)} %get-tuple-element.38), channel_id=1, source_target_pairs={{1,0},{2,1},{3,2},{5,4},{6,5},{7,6},{9,8},{10,9},{11,10},{13,12},{... | collective-permute-start | bytes 245768 | tf_op jit(solution)/shard_map/ppermute | solution.py:19
  207.3 8.6 %collective-permute-start.6 = (bf16[1,32,10,1,128]{4,1,3,2,0:T(8,128)(2,1)S(1)}, bf16[1,32,10,1,128]{4,1,3,2,0:T(8,128)(2,1)S(1)}, u32[]{:S(2)}, u32[]{:S(2)}) collective-permute-start(bf16[1,32,10,1,128]{4,1,3,2,0:T(8,128)(2,1)S(1)} %get-tuple-element.43), channel_id=1, source_target_pairs={{0,1},{1,2},{2,3},{4,5},{5,6},{6,7},{8,9},{9,10},{10,11},{12,13},{... | collective-permute-start | bytes 245768 | tf_op jit(solution)/shard_map/ppermute | solution.py:18
  211.9 6.3 %collective-permute-start.7 = (bf16[1,32,10,1,128]{4,1,3,2,0:T(8,128)(2,1)S(1)}, bf16[1,32,10,1,128]{4,1,3,2,0:T(8,128)(2,1)S(1)}, u32[]{:S(2)}, u32[]{:S(2)}) collective-permute-start(bf16[1,32,10,1,128]{4,1,3,2,0:T(8,128)(2,1)S(1)} %get-tuple-element.44), channel_id=1, source_target_pairs={{1,0},{2,1},{3,2},{5,4},{6,5},{7,6},{9,8},{10,9},{11,10},{13,12},{... | collective-permute-start | bytes 245768 | tf_op jit(solution)/shard_map/ppermute | solution.py:19
  (24 other events, 79.3 us)
Sparse Core Ops, SparseCore 0:
  257.3 129.5 all-reduce.9
where the time goes:
time: 403 us; the launch traced here: 398 us
  blocking collectives  126 us (31%)
  waiting for transfers between devices  122 us (30%)
  matrix products  66.3 us (16%)
  starting transfers between devices  43.5 us (11%)
  other arithmetic  19.3 us (5%)
  between operations  15.2 us (4%)
  local copies, waits for them, and re-layouts  5.44 us (1%)
    psum x1, waiting for transfers between devices, reduce_filters(): return lax.psum(tuple(filters), ('dp', 'sx', 'sy'))  119 us
    psum x2, blocking collectives, norm_backward(): lax.psum((local_sum(slope_grad), local_sum(slope_grad * centered)), ('dp'...  84.1 us
    dot_general x54, matrix products, back_project(): jnp.einsum('co,boxyz->bcxyz', weight[shift_x, shift_y, shift_z], piece, p...  49.5 us
    psum x1, blocking collectives, per_device(): lax.psum((local_sum(saved_one), local_sum(saved_one * saved_one), local_s...  42 us
    ppermute x8, starting transfers between devices, extended_2(): before = lax.ppermute(last, axis, up)  32.6 us
    dot_general x54, matrix products, filter_terms(): jnp.einsum('bcxyz,boxyz->co', piece, gradient, preferred_element_type=jnp...  16.8 us
    ppermute x8, starting transfers between devices, extended_2(): after = lax.ppermute(first, axis, down)  10.8 us
  transfers between devices with their start and end apart: 17, of which 3 were waited for; matrix products, arithmetic and copies ran while one was open for 17% of the time, Pallas kernels for 0%

commit v1 on v0

v1 whole, which is shorter than its diff:
```python
import functools
import math

import jax
import jax.numpy as jnp
from jax import lax
from jax.experimental import pallas as pl
from jax.experimental.pallas import tpu as pltpu
from jax.sharding import PartitionSpec as P

epsilon = 1e-05
AXES = ("dp", "sx", "sy")
NT = (((1,), (1,)), ((), ()))
F32 = jnp.float32
BF16 = jnp.bfloat16


def body(sizes, cells, c1, c2, ug, vol, w1, w2, g1, b1, g2, b2,
         out, filt, small,
         n1, n2, sl, d1, act, volp, grad, facc, ar, rb, og,
         ar_send, ar_recv, h_send, h_recv, rs_send, rs_recv, ag_send, ag_recv):
    n_dp, n_sx, n_sy = sizes
    n = n_dp * n_sx * n_sy
    ch, nx, ny, nz = c1.shape
    rows = ny * ch
    tiles = facc.shape[1]
    per = rb.shape[2]
    owners = tiles // per
    i_dp, i_sx, i_sy = [lax.axis_index(a) for a in AXES]
    me = (i_dp * n_sx + i_sx) * n_sy + i_sy

    def device(j):
        return (j // (n_sx * n_sy), (j // n_sy) % n_sx, j % n_sy)

    barrier = pltpu.get_barrier_semaphore()

    @pl.loop(1, n)
    def _(i):
        pl.semaphore_signal(barrier, inc=1, device_id=device((me + i) % n),
                            device_id_type=pl.DeviceIdType.MESH)

    r_i = lax.broadcasted_iota(jnp.int32, (rows, rows), 0)
    c_i = lax.broadcasted_iota(jnp.int32, (rows, rows), 1)
    perm = (c_i == (r_i % ch) * ny + r_i // ch).astype(F32).astype(BF16)
    back = (r_i == (c_i % ch) * ny + c_i // ch).astype(F32).astype(BF16)
    lane = lax.broadcasted_iota(jnp.int32, (ch, 128), 1)
    sub = lax.broadcasted_iota(jnp.int32, (ch, 128), 0)

    def load(ref, x):
        v = ref[:, x].astype(F32).reshape(rows, nz).astype(BF16)
        return jnp.dot(perm, v, preferred_element_type=F32)

    def per_channel(v):
        return jnp.sum(v.reshape(ny, ch, nz), axis=0)

    def tall(col):
        return jnp.concatenate([jnp.broadcast_to(col, (ch, nz))] * ny, axis=0)

    def column(row, q):
        wide = jnp.broadcast_to(row, (ch, 128))
        return jnp.sum(jnp.where(lane == sub + q * ch, wide, 0.0), axis=1, keepdims=True)

    def param(ref):
        wide = jnp.broadcast_to(ref[...], (ch, ch))
        return jnp.sum(jnp.where(lane[:, :ch] == sub[:, :ch], wide, 0.0), axis=1, keepdims=True)

    def start_sum(r, parts):
        parts = list(parts) + [jnp.zeros((ch, nz), F32)] * (128 // ch - len(parts))
        row = lax.dot_general(jnp.ones((8, nz), F32), jnp.concatenate(parts, axis=0), NT,
                              precision=lax.Precision.HIGHEST, preferred_element_type=F32)
        ar[r, me] = row[0:1]

        @pl.loop(1, n)
        def _(i):
            pltpu.make_async_remote_copy(
                ar.at[r, me], ar.at[r, me], ar_send.at[r], ar_recv.at[r],
                device_id=device((me + i) % n), device_id_type=pl.DeviceIdType.MESH).start()

    def end_sum(r):
        span = ar.at[r, pl.ds(0, n - 1)]
        pltpu.make_async_copy(span, span, ar_recv.at[r]).wait()
        pltpu.make_async_copy(span, span, ar_send.at[r]).wait()
        return jnp.sum(ar[r], axis=0)

    dirs = [(a, b) for a in (-1, 0, 1) for b in (-1, 0, 1) if (a, b) != (0, 0)]

    def side(step, extent, sending):
        if step == 0:
            return pl.ds(1, extent)
        if sending:
            return pl.ds(extent if step > 0 else 1, 1)
        return pl.ds(0 if step > 0 else extent + 1, 1)

    def halo_copy(k, d):
        a, b = dirs[d]
        return pltpu.make_async_remote_copy(
            grad.at[k, side(a, nx, True), side(b, ny, True), 1],
            grad.at[k, side(a, nx, False), side(b, ny, False), 1],
            h_send.at[k, d], h_recv.at[k, d],
            device_id=(i_dp, jnp.clip(i_sx + a, 0, n_sx - 1), jnp.clip(i_sy + b, 0, n_sy - 1)),
            device_id_type=pl.DeviceIdType.MESH)

    def there(a, b):
        return ((i_sx + a >= 0) & (i_sx + a < n_sx) & (i_sy + b >= 0) & (i_sy + b < n_sy))

    def start_halo(k):
        for d, (a, b) in enumerate(dirs):
            @pl.when(there(a, b))
            def _():
                halo_copy(k, d).start()

    lane_z = lax.broadcasted_iota(jnp.int32, (rows, nz), 1)

    def shifted(v):
        m = lane_z[: v.shape[0]]
        left = jnp.where(m == 0, 0.0, pltpu.roll(v, 1, 1))
        right = jnp.where(m == nz - 1, 0.0, pltpu.roll(v, nz - 1, 1))
        return left.astype(BF16), right.astype(BF16)

    def end_halo(k):
        for d, (a, b) in enumerate(dirs):
            @pl.when(there(-a, -b))
            def _():
                halo_copy(k, d).wait_recv()

            @pl.when(there(a, b))
            def _():
                halo_copy(k, d).wait_send()

        @pl.loop(0, ny)
        def _(i):
            for at in ((0, i + 1), (nx + 1, i + 1)):
                left, right = shifted(grad[k, at[0], at[1], 1].astype(F32))
                grad[k, at[0], at[1], 0] = left
                grad[k, at[0], at[1], 2] = right

        @pl.loop(0, nx + 2)
        def _(i):
            for at in (0, ny + 1):
                left, right = shifted(grad[k, i, at, 1].astype(F32))
                grad[k, i, at, 0] = left
                grad[k, i, at, 2] = right

    def project(w, k, x):
        pieces = []
        for y in range(ny):
            g = jnp.concatenate(
                [grad[k, x + a, y : y + 3].reshape(9 * ch, nz) for a in range(3)], axis=0)
            pieces.append(jnp.dot(w[...], g, preferred_element_type=F32))
        return jnp.concatenate(pieces, axis=0)

    def filters(k, u):
        facc[k] = jnp.zeros(facc.shape[1:], F32)

        @pl.loop(0, nx + 2)
        def _(x):
            lhs = jnp.concatenate(
                [grad[k, x, y : y + 3].reshape(9 * ch, nz) for y in range(ny)], axis=1)
            rhs = jnp.concatenate(
                [u[y, pl.ds(x, 3)].reshape(3 * ch, nz) for y in range(ny)], axis=1)
            rhs = jnp.concatenate([rhs, jnp.zeros((128 - 3 * ch, ny * nz), BF16)], axis=0)
            r = lax.dot_general(lhs, rhs, NT, preferred_element_type=F32)
            facc[k] += r.reshape(facc.shape[1:])

    def start_scatter(k):
        @pl.loop(0, owners)
        def _(i):
            j = (me + i) % owners

            @pl.when(j != me)
            def _():
                pltpu.make_async_remote_copy(
                    facc.at[k, pl.ds(j * per, per)], rb.at[k, me], rs_send.at[k], rs_recv.at[k],
                    device_id=device(j), device_id_type=pl.DeviceIdType.MESH).start()

    def wait_bytes(ref, sem):
        pltpu.make_async_copy(ref, ref, sem).wait()

    def start_gather(k):
        @pl.when(me < owners)
        def _():
            mine = pl.ds(me * per, per)
            rb[k, me] = facc[k, mine]
            wait_bytes(rb.at[k, pl.ds(0, n - 1)], rs_recv.at[k])
            og[k, mine] = jnp.sum(rb[k], axis=0) * (1.0 / math.sqrt(cells))

            @pl.loop(1, n)
            def _(i):
                pltpu.make_async_remote_copy(
                    og.at[k, mine], og.at[k, mine], ag_send.at[k], ag_recv.at[k],
                    device_id=device((me + i) % n), device_id_type=pl.DeviceIdType.MESH).start()

    def end_gather(k):
        @pl.when(me < owners)
        def _():
            wait_bytes(facc.at[k, pl.ds(0, (owners - 1) * per)], rs_send.at[k])
            wait_bytes(og.at[k, pl.ds(0, (owners - 1) * per)], ag_recv.at[k])
            wait_bytes(rb.at[k, pl.ds(0, n - 1)], ag_send.at[k])

        @pl.when(me >= owners)
        def _():
            wait_bytes(facc.at[k], rs_send.at[k])
            wait_bytes(og.at[k], ag_recv.at[k])

        filt[k] = og[k]

    zero = jnp.zeros((ch, nz), F32)

    def moments(x, acc):
        v1, v2 = load(c1, x), load(c2, x)
        n1[x], n2[x] = v1, v2
        sl[x] = load(ug, x)
        new = (v1, v1 * v1, v2, v2 * v2)
        return tuple(a + per_channel(v) for a, v in zip(acc, new))

    parts = lax.fori_loop(0, nx, moments, (zero,) * 4)
    for k in range(2):
        grad[k, pl.ds(0, 1)] = jnp.zeros((1,) + grad.shape[2:], BF16)
        grad[k, pl.ds(nx + 1, 1)] = jnp.zeros((1,) + grad.shape[2:], BF16)
        for at in (0, ny + 1):
            grad[k, :, at] = jnp.zeros((nx + 2,) + grad.shape[3:], BF16)
    pl.semaphore_wait(barrier, n - 1)
    start_sum(0, parts)

    for u in (act, volp):
        for at in (0, nx + 2):
            u[:, pl.ds(at, 2)] = jnp.zeros((ny, 2, ch, nz), BF16)

    @pl.loop(0, nx)
    def _(x):
        volp[:, x + 2] = load(vol, x).astype(BF16).reshape(ny, ch, nz)

    total = end_sum(0)

    def norm(q):
        mean = column(total, q) / cells
        spread = column(total, q + 1) / cells - mean * mean
        return mean, lax.rsqrt(spread + epsilon)

    mean1, inv1 = norm(0)
    mean2, inv2 = norm(2)
    gain1, bias1, gain2, bias2 = param(g1), param(b1), param(g2), param(b2)
    mean1_t, inv1_t, gain1_t, bias1_t = tall(mean1), tall(inv1), tall(gain1), tall(bias1)
    mean2_t, inv2_t, gain2_t, bias2_t = tall(mean2), tall(inv2), tall(gain2), tall(bias2)

    def slope_two(x, acc):
        cent = (n2[x] - mean2_t) * inv2_t
        v = gain2_t * cent + bias2_t
        s = jax.nn.sigmoid(v)
        slope = sl[x] * (s * (1.0 + v * (1.0 - s)))
        n2[x] = cent
        sl[x] = slope
        return acc[0] + per_channel(slope), acc[1] + per_channel(slope * cent)

    start_sum(1, lax.fori_loop(0, nx, slope_two, (zero, zero)))

    @pl.loop(0, nx)
    def _(x):
        cent = (n1[x] - mean1_t) * inv1_t
        v = gain1_t * cent + bias1_t
        s = jax.nn.sigmoid(v)
        n1[x] = cent
        d1[x] = s * (1.0 + v * (1.0 - s))
        act[:, x + 2] = (v * s).astype(BF16).reshape(ny, ch, nz)

    def make_grad(k, row, cent, scale):
        bsum, gsum = tall(column(row, 0) / cells), tall(column(row, 1) / cells)
        scale = tall(scale)

        @pl.loop(0, nx)
        def _(x):
            v = scale * (sl[x] - bsum - cent[x] * gsum)
            left, right = shifted(v)
            for kz, part in enumerate((left, v.astype(BF16), right)):
                grad[k, x + 1, pl.ds(1, ny), kz] = part.reshape(ny, ch, nz)

    factor = 1.0 / math.sqrt(cells)
    row = end_sum(1)
    small[0:1] = row * factor
    make_grad(0, row, n2, gain2 * inv2)
    start_halo(0)
    end_halo(0)

    def slope_one(x, acc):
        slope = project(w2, 0, x) * d1[x]
        sl[x] = slope
        return acc[0] + per_channel(slope), acc[1] + per_channel(slope * n1[x])

    start_sum(2, lax.fori_loop(0, nx, slope_one, (zero, zero)))
    filters(0, act)
    start_scatter(0)
    row = end_sum(2)
    small[1:2] = row * factor
    make_grad(1, row, n1, gain1 * inv1)
    start_halo(1)
    start_gather(0)
    end_halo(1)
    filters(1, volp)
    start_scatter(1)

    @pl.loop(0, nx)
    def _(x):
        v = project(w1, 1, x).astype(BF16)
        out[:, x] = jnp.dot(back, v, preferred_element_type=F32).reshape(ch, ny, nz).astype(BF16)

    start_gather(1)
    end_gather(0)
    end_gather(1)


def per_device(volume, conv_one, conv_two, upper_grad, weight_one, weight_two,
               gain_one, bias_one, gain_two, bias_two):
    sizes = tuple(lax.axis_size(a) for a in AXES)
    n = math.prod(sizes)
    _, ch, nx, ny, nz = volume.shape
    cells = float(volume.shape[0] * nx * ny * nz * n)
    tiles = 9 * ch // 8
    per = -(-tiles // n)
    while tiles % per:
        per += 1

    def flat(w):
        return jnp.transpose(w[::-1, ::-1, ::-1], (3, 0, 1, 2, 4)).reshape(ch, 27 * ch)

    vmem = pl.BlockSpec(memory_space=pltpu.VMEM)
    dma = pltpu.SemaphoreType.DMA
    big = pltpu.VMEM((nx, ny * ch, nz), F32)
    pad_u = pltpu.VMEM((ny, nx + 4, ch, nz), BF16)
    out, filt, small = pl.pallas_call(
        functools.partial(body, sizes, cells),
        name="section_backward",
        out_shape=(
            jax.ShapeDtypeStruct((ch, nx, ny, nz), BF16),
            jax.ShapeDtypeStruct((2, tiles, 8, 128), F32),
            jax.ShapeDtypeStruct((8, 128), F32),
        ),
        in_specs=[vmem] * 10,
        out_specs=(vmem,) * 3,
        scratch_shapes=[
            big, big, big, big, pad_u, pad_u,
            pltpu.VMEM((2, nx + 2, ny + 2, 3, ch, nz), BF16),
            pltpu.VMEM((2, tiles, 8, 128), F32),
            pltpu.VMEM((3, n, 1, 128), F32),
            pltpu.VMEM((2, n, per, 8, 128), F32),
            pltpu.VMEM((2, tiles, 8, 128), F32),
            dma((3,)), dma((3,)), dma((2, 8)), dma((2, 8)),
            dma((2,)), dma((2,)), dma((2,)), dma((2,)),
        ],
        compiler_params=pltpu.CompilerParams(
            collective_id=0, has_side_effects=True, vmem_limit_bytes=60 * 1024 * 1024),
    )(conv_one[0], conv_two[0], upper_grad[0], volume[0], flat(weight_one), flat(weight_two),
      gain_one[None], bias_one[None], gain_two[None], bias_two[None])

    def unflat(f):
        f = f.reshape(3, 3, ch, 128)[..., : 3 * ch].reshape(3, 3, ch, 3, ch)
        return jnp.transpose(f, (3, 0, 1, 4, 2))[:, ::-1, ::-1]

    return (out[None], unflat(filt[1]), unflat(filt[0]),
            small[1, ch : 2 * ch], small[1, :ch], small[0, ch : 2 * ch], small[0, :ch])


def solution(mesh):
    block = P("dp", None, "sx", "sy", None)
    return jax.shard_map(
        per_device,
        mesh=mesh,
        in_specs=(block,) * 4 + (P(),) * 6,
        out_specs=(block,) + (P(),) * 6,
        check_vma=False,
    )
```

time: 403 us -> 68.4 us (0.17); the launches traced: 398 us -> 68.1 us
  blocking collectives: 126 us -> 0 us
  waiting for transfers between devices: 122 us -> 0 us
  matrix products: 66.3 us -> 0 us
  Pallas kernels: 0 us -> 58.6 us
  starting transfers between devices: 43.5 us -> 0 us
  other arithmetic: 19.3 us -> 0 us
  between operations: 15.2 us -> 0.72 us
    psum x3 -> x0, blocking collectives: 126 us -> none  [the longest x2 84.1 us: norm_backward(): lax.psum((local_sum(slope_grad), local_sum(slope_grad * centered)), ('dp'...]
    psum x1 -> x0, waiting for transfers between devices: 119 us -> none  [reduce_filters(): return lax.psum(tuple(filters), ('dp', 'sx', 'sy'))]
    dot_general x108 -> x0, matrix products: 66.3 us -> none  [the longest x54 49.5 us: back_project(): jnp.einsum('co,boxyz->bcxyz', weight[shift_x, shift_y, shift_z], piece, p...]
    pallas_call x0 -> x1, Pallas kernels: none -> 58.6 us  [per_device(): pl.pallas_call(functools.partial(body, sizes, cells), name='section_backw...]
    ppermute x16 -> x0, starting transfers between devices: 43.4 us -> none  [the longest x8 32.6 us: extended_2(): before = lax.ppermute(last, axis, up)]
    concatenate x7 -> x0, other arithmetic: 6.08 us -> none  [extended_2(): array = jnp.concatenate([before, array, after], axis=dim)]
    mul x7 -> x0, other arithmetic: 5.83 us -> none  [the longest x1 1.81 us: per_device(): filter_two * factor]
    reduce_sum x3 -> x0, other arithmetic: 5.23 us -> none  [local_sum(): return jnp.sum(values, axis=(0, 2, 3, 4))]
  transfers between devices with their start and end apart: 17 -> 0, of which waited for: 3 -> 0; matrix products, arithmetic and copies ran while one was open for 17% -> 0% of each run, Pallas kernels for 0% -> 0%
where the time goes in v1:
time: 68.4 us; the launch traced here: 68.1 us
  Pallas kernels  58.6 us (86%)
  local copies, waits for them, and re-layouts  8.76 us (13%)
  between operations  0.72 us (1%)
    pallas_call x1, Pallas kernels, per_device(): pl.pallas_call(functools.partial(body, sizes, cells), name='section_backw...  58.6 us
    unnamed x9, local copies, waits for them, and re-layouts  3.57 us
    reshape x2, local copies, waits for them, and re-layouts, flat(): jnp.transpose(w[::-1, ::-1, ::-1], (3, 0, 1, 2, 4)).reshape(ch, 27 * ch)  1.63 us

profile of v1, /device:TPU:0, one launch (start us, length us, event | category | flops | bytes accessed | tf_op | source)
XLA Modules:
  0.0 68.1 jit_solution(4011849917307759887)
XLA Ops:
  0.6 1.0 %reverse_bitcast_fusion.1 = bf16[32,3,3,3,32]{4,0,3,2,1:T(8,128)(2,1)S(1)} fusion(bf16[3,3,3,32,32]{4,3,2,1,0:T(8,128)(2,1)} %param.14), kind=kLoop, calls=%fused_computation.1 | loop fusion | bytes 110592 | tf_op jit(solution)/shard_map/transpose | solution.py:323
  1.6 0.2 copy.19
  1.7 0.0 copy-start.1
  1.8 0.8 %reshape.26.w1 = bf16[32,864]{1,0:T(8,128)(2,1)} reshape(bf16[32,3,3,3,32]{4,3,2,1,0:T(4,128)(2,1)S(1)} %copy.19) | data formatting | bytes 110592 | tf_op jit(solution)/shard_map/reshape | solution.py:323
  2.6 0.1 copy-done.1
  2.7 0.2 copy.20
  2.9 0.8 %reshape.27.w2 = bf16[32,864]{1,0:T(8,128)(2,1)} reshape(bf16[32,3,3,3,32]{4,3,2,1,0:T(4,128)(2,1)S(1)} %copy.20) | data formatting | bytes 110592 | tf_op jit(solution)/shard_map/reshape | solution.py:323
  3.7 58.6 %section_backward.1 = (bf16[32,8,8,128]{3,2,1,0:T(8,128)(2,1)}, f32[2,36,8,128]{3,2,1,0:T(8,128)}, f32[8,128]{1,0:T(8,128)}) custom-call(bf16[32,8,8,128]{3,2,1,0:T(8,128)(2,1)} %bitcast.35, bf16[32,8,8,128]{3,2,1,0:T(8,128)(2,1)} %bitcast.36, bf16[32,8,8,128]{3,2,1,0:T(8,128)(2,1)} %bitcast.37, bf16[32,8,8,128]{3,2,1,0:T(8,128)(2,1)} %bitcast.38, ...), custom_call_target="tpu_custom_call" | custom-call | tf_op jit(solution)/shard_map/section_backward/pallas_call | solution.py:329
  62.3 0.0 copy-start.2
  62.3 0.7 copy-done.2
  63.0 0.6 slice_bitcast_fusion
  63.6 1.0 %fusion = (f32[1,36,8,128]{3,2,1,0:T(8,128)S(1)}, f32[1,36,8,128]{3,2,1,0:T(8,128)S(1)}) fusion(f32[2,36,8,128]{3,2,1,0:T(8,128)} %get-tuple-element.11), kind=kLoop, calls=%fused_computation.6 | loop fusion | bytes 589824 | tf_op jit(solution)/shard_map/slice | solution.py:358
  64.6 0.2 reshape.28
  64.9 0.1 rev.14
  65.0 1.0 %copy.21 = f32[3,3,3,32,32]{4,3,2,1,0:T(8,128)} copy(f32[3,3,3,32,32]{3,0,4,2,1:T(4,128)S(1)} %rev.14) | data formatting | bytes 221184
  65.9 0.2 reshape.29
  66.2 0.1 rev.15
  66.3 0.0 copy-start
  66.3 1.0 %copy.22 = f32[3,3,3,32,32]{4,3,2,1,0:T(8,128)} copy(f32[3,3,3,32,32]{3,0,4,2,1:T(4,128)S(1)} %rev.15) | data formatting | bytes 221184
  67.3 0.1 copy-done
  67.3 0.8 %copy.24 = bf16[1,32,8,8,128]{4,3,2,1,0:T(8,128)(2,1)} copy(bf16[1,32,8,8,128]{4,3,2,1,0:T(8,128)(2,1)S(1)} %bitcast.39) | data formatting | bytes 1048576
  (1 shorter events, 0.0 us)
Async XLA Ops:
  1.7 0.9 %copy-start.1 = (bf16[3,3,3,32,32]{4,3,2,1,0:T(8,128)(2,1)S(1)}, bf16[3,3,3,32,32]{4,3,2,1,0:T(8,128)(2,1)}, u32[]{:S(2)}) copy-start(bf16[3,3,3,32,32]{4,3,2,1,0:T(8,128)(2,1)} %param.15) | copy-start | bytes 165892
  62.3 0.7 copy-start.2
  66.3 1.0 %copy-start = (bf16[32,8,8,128]{3,2,1,0:T(8,128)(2,1)S(1)}, bf16[32,8,8,128]{3,2,1,0:T(8,128)(2,1)}, u32[]{:S(2)}) copy-start(bf16[32,8,8,128]{3,2,1,0:T(8,128)(2,1)} %get-tuple-element.10) | copy-start | bytes 1572868

commit v2 on v1

--- a/solution.py
+++ b/solution.py
@@ -16,8 +16,8 @@
 
 
 def body(sizes, cells, c1, c2, ug, vol, w1, w2, g1, b1, g2, b2,
-         out, filt, small,
-         n1, n2, sl, d1, act, volp, grad, facc, ar, rb, og,
+         out, og, small,
+         n1, n2, sl, d1, act, volp, grad, facc, ar, rb, wt, hx, hc, hs,
          ar_send, ar_recv, h_send, h_recv, rs_send, rs_recv, ag_send, ag_recv):
     n_dp, n_sx, n_sy = sizes
     n = n_dp * n_sx * n_sy
@@ -29,20 +29,30 @@
     i_dp, i_sx, i_sy = [lax.axis_index(a) for a in AXES]
     me = (i_dp * n_sx + i_sx) * n_sy + i_sy
 
-    def device(j):
-        return (j // (n_sx * n_sy), (j // n_sy) % n_sx, j % n_sy)
+    def each_peer(use):
+        def step(_, at):
+            a, b, c = at
+            c = c + 1
+            b = jnp.where(c == n_sy, b + 1, b)
+            c = jnp.where(c == n_sy, 0, c)
+            a = jnp.where(b == n_sx, a + 1, a)
+            b = jnp.where(b == n_sx, 0, b)
+            a = jnp.where(a == n_dp, 0, a)
+            use((a, b, c))
+            return a, b, c
+
+        lax.fori_loop(0, n - 1, step, (i_dp, i_sx, i_sy))
 
     barrier = pltpu.get_barrier_semaphore()
 
-    @pl.loop(1, n)
-    def _(i):
-        pl.semaphore_signal(barrier, inc=1, device_id=device((me + i) % n),
+    @each_peer
+    def _(peer):
+        pl.semaphore_signal(barrier, inc=1, device_id=peer,
                             device_id_type=pl.DeviceIdType.MESH)
 
     r_i = lax.broadcasted_iota(jnp.int32, (rows, rows), 0)
     c_i = lax.broadcasted_iota(jnp.int32, (rows, rows), 1)
     perm = (c_i == (r_i % ch) * ny + r_i // ch).astype(F32).astype(BF16)
-    back = (r_i == (c_i % ch) * ny + c_i // ch).astype(F32).astype(BF16)
     lane = lax.broadcasted_iota(jnp.int32, (ch, 128), 1)
     sub = lax.broadcasted_iota(jnp.int32, (ch, 128), 0)
 
@@ -70,11 +80,11 @@
                               precision=lax.Precision.HIGHEST, preferred_element_type=F32)
         ar[r, me] = row[0:1]
 
-        @pl.loop(1, n)
-        def _(i):
+        @each_peer
+        def _(peer):
             pltpu.make_async_remote_copy(
                 ar.at[r, me], ar.at[r, me], ar_send.at[r], ar_recv.at[r],
-                device_id=device((me + i) % n), device_id_type=pl.DeviceIdType.MESH).start()
+                device_id=peer, device_id_type=pl.DeviceIdType.MESH).start()
 
     def end_sum(r):
         span = ar.at[r, pl.ds(0, n - 1)]
@@ -94,8 +104,8 @@
     def halo_copy(k, d):
         a, b = dirs[d]
         return pltpu.make_async_remote_copy(
-            grad.at[k, side(a, nx, True), side(b, ny, True), 1],
-            grad.at[k, side(a, nx, False), side(b, ny, False), 1],
+            hx.at[k, side(a, nx, True), side(b, ny, True)],
+            hx.at[k, side(a, nx, False), side(b, ny, False)],
             h_send.at[k, d], h_recv.at[k, d],
             device_id=(i_dp, jnp.clip(i_sx + a, 0, n_sx - 1), jnp.clip(i_sy + b, 0, n_sy - 1)),
             device_id_type=pl.DeviceIdType.MESH)
@@ -109,7 +119,7 @@
             def _():
                 halo_copy(k, d).start()
 
-    lane_z = lax.broadcasted_iota(jnp.int32, (rows, nz), 1)
+    lane_z = lax.broadcasted_iota(jnp.int32, (rows + 2 * ch, nz), 1)
 
     def shifted(v):
         m = lane_z[: v.shape[0]]
@@ -127,26 +137,42 @@
             def _():
                 halo_copy(k, d).wait_send()
 
-        @pl.loop(0, ny)
-        def _(i):
-            for at in ((0, i + 1), (nx + 1, i + 1)):
-                left, right = shifted(grad[k, at[0], at[1], 1].astype(F32))
-                grad[k, at[0], at[1], 0] = left
-                grad[k, at[0], at[1], 2] = right
-
-        @pl.loop(0, nx + 2)
-        def _(i):
-            for at in (0, ny + 1):
-                left, right = shifted(grad[k, i, at, 1].astype(F32))
-                grad[k, i, at, 0] = left
-                grad[k, i, at, 2] = right
-
-    def project(w, k, x):
+    rims = [(0, None, ny + 2), (nx + 1, None, ny + 2), (None, 0, nx), (None, ny + 1, nx)]
+
+    def rim_of(q, i):
+        x, y, m = rims[i]
+        return (hx[q, x] if y is None else hx[q, pl.ds(1, nx), y]).astype(F32)
+
+    def inside(i):
+        x, y, m = rims[i]
+        at = lax.broadcasted_iota(jnp.int32, (m, ch, nz), 0)
+        if y is None:
+            fixed, size, low, limit = i_sx * nx + x - 1, n_sx * nx, i_sy * ny - 1, n_sy * ny
+        else:
+            fixed, size, low, limit = i_sy * ny + y - 1, n_sy * ny, 0, nx + 1
+        bound = jnp.where((fixed >= 0) & (fixed < size), 0, limit)
+        return (at + low >= bound) & (at + low < limit)
+
+    def rim_grad(k, bsum, gsum, scale):
+        for i, (x, y, m) in enumerate(rims):
+            slope = hs[i, pl.ds(0, m)] if k == 0 else rim_of(3, i)
+            v = scale * (slope - bsum - hc[k, i, pl.ds(0, m)] * gsum)
+            v = jnp.where(inside(i), v, 0.0).reshape(m * ch, nz)
+            left, right = shifted(v)
+            for kz, part in enumerate((left, v.astype(BF16), right)):
+                part = part.reshape(m, ch, nz)
+                if y is None:
+                    grad[k, x, :, kz] = part
+                else:
+                    grad[k, pl.ds(1, nx), y, kz] = part
+
+    def project(k, x):
+        w = wt[k, :, pl.ds(0, 27 * ch)]
         pieces = []
         for y in range(ny):
             g = jnp.concatenate(
                 [grad[k, x + a, y : y + 3].reshape(9 * ch, nz) for a in range(3)], axis=0)
-            pieces.append(jnp.dot(w[...], g, preferred_element_type=F32))
+            pieces.append(jnp.dot(w, g, preferred_element_type=F32))
         return jnp.concatenate(pieces, axis=0)
 
     def filters(k, u):
@@ -163,15 +189,15 @@
             facc[k] += r.reshape(facc.shape[1:])
 
     def start_scatter(k):
-        @pl.loop(0, owners)
-        def _(i):
-            j = (me + i) % owners
-
-            @pl.when(j != me)
+        @each_peer
+        def _(peer):
+            j = (peer[0] * n_sx + peer[1]) * n_sy + peer[2]
+
+            @pl.when(j < owners)
             def _():
                 pltpu.make_async_remote_copy(
                     facc.at[k, pl.ds(j * per, per)], rb.at[k, me], rs_send.at[k], rs_recv.at[k],
-                    device_id=device(j), device_id_type=pl.DeviceIdType.MESH).start()
+                    device_id=peer, device_id_type=pl.DeviceIdType.MESH).start()
 
     def wait_bytes(ref, sem):
         pltpu.make_async_copy(ref, ref, sem).wait()
@@ -184,11 +210,11 @@
             wait_bytes(rb.at[k, pl.ds(0, n - 1)], rs_recv.at[k])
             og[k, mine] = jnp.sum(rb[k], axis=0) * (1.0 / math.sqrt(cells))
 
-            @pl.loop(1, n)
-            def _(i):
+            @each_peer
+            def _(peer):
                 pltpu.make_async_remote_copy(
                     og.at[k, mine], og.at[k, mine], ag_send.at[k], ag_recv.at[k],
-                    device_id=device((me + i) % n), device_id_type=pl.DeviceIdType.MESH).start()
+                    device_id=peer, device_id_type=pl.DeviceIdType.MESH).start()
 
     def end_gather(k):
         @pl.when(me < owners)
@@ -202,25 +228,33 @@
             wait_bytes(facc.at[k], rs_send.at[k])
             wait_bytes(og.at[k], ag_recv.at[k])
 
-        filt[k] = og[k]
-
     zero = jnp.zeros((ch, nz), F32)
 
     def moments(x, acc):
         v1, v2 = load(c1, x), load(c2, x)
         n1[x], n2[x] = v1, v2
-        sl[x] = load(ug, x)
+        v3 = load(ug, x)
+        sl[x] = v3
+        for q, v in enumerate((v2, v3, v1)):
+            hx[q, x + 1, pl.ds(1, ny)] = v.astype(BF16).reshape(ny, ch, nz)
         new = (v1, v1 * v1, v2, v2 * v2)
         return tuple(a + per_channel(v) for a, v in zip(acc, new))
 
     parts = lax.fori_loop(0, nx, moments, (zero,) * 4)
-    for k in range(2):
-        grad[k, pl.ds(0, 1)] = jnp.zeros((1,) + grad.shape[2:], BF16)
-        grad[k, pl.ds(nx + 1, 1)] = jnp.zeros((1,) + grad.shape[2:], BF16)
-        for at in (0, ny + 1):
-            grad[k, :, at] = jnp.zeros((nx + 2,) + grad.shape[3:], BF16)
     pl.semaphore_wait(barrier, n - 1)
     start_sum(0, parts)
+    start_halo(0)
+    start_halo(1)
+
+    group = 128 // ch
+    for k, w in enumerate((w2, w1)):
+        for first in range(0, 27, group):
+            total = jnp.zeros((ch, 128), F32)
+            for t in range(first, min(first + group, 27)):
+                r = 26 - t
+                pick = (lane == sub + (t - first) * ch).astype(F32).astype(BF16)
+                total += jnp.dot(w[r // 9, r // 3 % 3, r % 3], pick, preferred_element_type=F32)
+            wt[k, :, pl.ds(first * ch, 128)] = total.astype(BF16)
 
     for u in (act, volp):
         for at in (0, nx + 2):
@@ -253,6 +287,7 @@
         return acc[0] + per_channel(slope), acc[1] + per_channel(slope * cent)
 
     start_sum(1, lax.fori_loop(0, nx, slope_two, (zero, zero)))
+    start_halo(2)
 
     @pl.loop(0, nx)
     def _(x):
@@ -264,8 +299,9 @@
         act[:, x + 2] = (v * s).astype(BF16).reshape(ny, ch, nz)
 
     def make_grad(k, row, cent, scale):
-        bsum, gsum = tall(column(row, 0) / cells), tall(column(row, 1) / cells)
-        scale = tall(scale)
+        bsum, gsum = column(row, 0) / cells, column(row, 1) / cells
+        rim_grad(k, wide(bsum), wide(gsum), wide(scale))
+        bsum, gsum, scale = tall(bsum), tall(gsum), tall(scale)
 
         @pl.loop(0, nx)
         def _(x):
@@ -274,38 +310,71 @@
             for kz, part in enumerate((left, v.astype(BF16), right)):
                 grad[k, x + 1, pl.ds(1, ny), kz] = part.reshape(ny, ch, nz)
 
+    def wide(col):
+        return jnp.broadcast_to(col, (ch, nz))[None]
+
+    end_halo(0)
+    end_halo(1)
+    for i in range(4):
+        m = rims[i][2]
+        cent = (rim_of(0, i) - wide(mean2)) * wide(inv2)
+        v = wide(gain2) * cent + wide(bias2)
+        s = jax.nn.sigmoid(v)
+        hc[0, i, pl.ds(0, m)] = cent
+        hs[i, pl.ds(0, m)] = rim_of(1, i) * (s * (1.0 + v * (1.0 - s)))
+
     factor = 1.0 / math.sqrt(cells)
     row = end_sum(1)
     small[0:1] = row * factor
     make_grad(0, row, n2, gain2 * inv2)
-    start_halo(0)
-    end_halo(0)
 
     def slope_one(x, acc):
-        slope = project(w2, 0, x) * d1[x]
+        slope = project(0, x) * d1[x]
         sl[x] = slope
+        hx[3, x + 1, pl.ds(1, ny)] = slope.astype(BF16).reshape(ny, ch, nz)
         return acc[0] + per_channel(slope), acc[1] + per_channel(slope * n1[x])
 
     start_sum(2, lax.fori_loop(0, nx, slope_one, (zero, zero)))
+    start_halo(3)
     filters(0, act)
     start_scatter(0)
+    end_halo(2)
+    for i in range(4):
+        hc[1, i, pl.ds(0, rims[i][2])] = (rim_of(2, i) - wide(mean1)) * wide(inv1)
     row = end_sum(2)
     small[1:2] = row * factor
+    end_halo(3)
     make_grad(1, row, n1, gain1 * inv1)
-    start_halo(1)
     start_gather(0)
-    end_halo(1)
     filters(1, volp)
     start_scatter(1)
 
     @pl.loop(0, nx)
     def _(x):
-        v = project(w1, 1, x).astype(BF16)
-        out[:, x] = jnp.dot(back, v, preferred_element_type=F32).reshape(ch, ny, nz).astype(BF16)
+        out[x] = project(1, x).astype(BF16)
 
     start_gather(1)
     end_gather(0)
     end_gather(1)
+
+
+def finish(rows_in, og, small, out, f1, f2, g1, b1, g2, b2):
+    ch, nx, ny, nz = out.shape
+    rows = ny * ch
+    r_i = lax.broadcasted_iota(jnp.int32, (rows, rows), 0)
+    c_i = lax.broadcasted_iota(jnp.int32, (rows, rows), 1)
+    back = (r_i == (c_i % ch) * ny + c_i // ch).astype(F32).astype(BF16)
+    for x in range(nx):
+        v = jnp.dot(back, rows_in[x], preferred_element_type=F32)
+        out[:, x] = v.reshape(ch, ny, nz).astype(BF16)
+    for k, f in enumerate((f2, f1)):
+        for b in range(9):
+            t = og[k, pl.ds(b * ch // 8, ch // 8)].reshape(ch, 128).T
+            for kx in range(3):
+                f[kx, 2 - b // 3, 2 - b % 3] = t[kx * ch : (kx + 1) * ch]
+    for r, (b, g) in enumerate(((b2, g2), (b1, g1))):
+        b[...] = small[r : r + 1, :ch]
+        g[...] = small[r : r + 1, ch : 2 * ch]
 
 
 def per_device(volume, conv_one, conv_two, upper_grad, weight_one, weight_two,
@@ -319,18 +388,15 @@
     while tiles % per:
         per += 1
 
-    def flat(w):
-        return jnp.transpose(w[::-1, ::-1, ::-1], (3, 0, 1, 2, 4)).reshape(ch, 27 * ch)
-
     vmem = pl.BlockSpec(memory_space=pltpu.VMEM)
     dma = pltpu.SemaphoreType.DMA
     big = pltpu.VMEM((nx, ny * ch, nz), F32)
     pad_u = pltpu.VMEM((ny, nx + 4, ch, nz), BF16)
-    out, filt, small = pl.pallas_call(
+    mid = pl.pallas_call(
         functools.partial(body, sizes, cells),
         name="section_backward",
         out_shape=(
-            jax.ShapeDtypeStruct((ch, nx, ny, nz), BF16),
+            jax.ShapeDtypeStruct((nx, ny * ch, nz), BF16),
             jax.ShapeDtypeStruct((2, tiles, 8, 128), F32),
             jax.ShapeDtypeStruct((8, 128), F32),
         ),
@@ -342,21 +408,28 @@
             pltpu.VMEM((2, tiles, 8, 128), F32),
             pltpu.VMEM((3, n, 1, 128), F32),
             pltpu.VMEM((2, n, per, 8, 128), F32),
-            pltpu.VMEM((2, tiles, 8, 128), F32),
-            dma((3,)), dma((3,)), dma((2, 8)), dma((2, 8)),
+            pltpu.VMEM((2, ch, -(-27 * ch // 128) * 128), BF16),
+            pltpu.VMEM((4, nx + 2, ny + 2, ch, nz), BF16),
+            pltpu.VMEM((2, 4, max(nx, ny) + 2, ch, nz), F32),
+            pltpu.VMEM((4, max(nx, ny) + 2, ch, nz), F32),
+            dma((3,)), dma((3,)), dma((4, 8)), dma((4, 8)),
             dma((2,)), dma((2,)), dma((2,)), dma((2,)),
         ],
         compiler_params=pltpu.CompilerParams(
             collective_id=0, has_side_effects=True, vmem_limit_bytes=60 * 1024 * 1024),
-    )(conv_one[0], conv_two[0], upper_grad[0], volume[0], flat(weight_one), flat(weight_two),
+    )(conv_one[0], conv_two[0], upper_grad[0], volume[0], weight_one, weight_two,
       gain_one[None], bias_one[None], gain_two[None], bias_two[None])
 
-    def unflat(f):
-        f = f.reshape(3, 3, ch, 128)[..., : 3 * ch].reshape(3, 3, ch, 3, ch)
-        return jnp.transpose(f, (3, 0, 1, 4, 2))[:, ::-1, ::-1]
-
-    return (out[None], unflat(filt[1]), unflat(filt[0]),
-            small[1, ch : 2 * ch], small[1, :ch], small[0, ch : 2 * ch], small[0, :ch])
+    vector = jax.ShapeDtypeStruct((1, ch), F32)
+    filt = jax.ShapeDtypeStruct(weight_one.shape, F32)
+    out, *rest = pl.pallas_call(
+        finish,
+        name="section_finish",
+        out_shape=(jax.ShapeDtypeStruct((ch, nx, ny, nz), BF16), filt, filt) + (vector,) * 4,
+        in_specs=[vmem] * 3,
+        out_specs=(vmem,) * 7,
+    )(*mid)
+    return (out[None], *rest[:2], *(v[0] for v in rest[2:]))
 
 
 def solution(mesh):

time: 68.4 us -> 55.4 us (0.81)
  local copies, waits for them, and re-layouts: 8.76 us -> 0 us
  Pallas kernels: 58.6 us -> 54.5 us
    pallas_call x1, Pallas kernels: 58.6 us -> 51.9 us  [per_device(): pl.pallas_call(functools.partial(body, sizes, cells), name='section_backw...]
    unnamed x9 -> x0, local copies, waits for them, and re-layouts: 3.57 us -> none
    pallas_call x0 -> x1, Pallas kernels: none -> 2.65 us  [per_device(): pl.pallas_call(finish, name='section_finish', out_shape=(jax.ShapeDtypeSt...]
    reshape x4 -> x0, local copies, waits for them, and re-layouts: 2.12 us -> none  [the longest x2 1.63 us: flat(): jnp.transpose(w[::-1, ::-1, ::-1], (3, 0, 1, 2, 4)).reshape(ch, 27 * ch)]
    transpose x4 -> x0, local copies, waits for them, and re-layouts: 1.27 us -> none  [flat(): jnp.transpose(w[::-1, ::-1, ::-1], (3, 0, 1, 2, 4)).reshape(ch, 27 * ch)]
    slice x1 -> x0, local copies, waits for them, and re-layouts: 1 us -> none  [per_device(): filt[0]]
where the time goes in v2:
time: 55.4 us; the launch traced here: 55.2 us
  Pallas kernels  54.5 us (98%)
  between operations  0.64 us (1%)
    pallas_call x1, Pallas kernels, per_device(): pl.pallas_call(functools.partial(body, sizes, cells), name='section_backw...  51.9 us
    pallas_call x1, Pallas kernels, per_device(): pl.pallas_call(finish, name='section_finish', out_shape=(jax.ShapeDtypeSt...  2.65 us

profile of v2, /device:TPU:0, one launch (start us, length us, event | category | flops | bytes accessed | tf_op | source)
XLA Modules:
  0.0 55.2 jit_solution(9911279592157704616)
XLA Ops:
  0.6 51.9 %section_backward.1 = (bf16[8,256,128]{2,1,0:T(8,128)(2,1)}, f32[2,36,8,128]{3,2,1,0:T(8,128)}, f32[8,128]{1,0:T(8,128)}) custom-call(bf16[32,8,8,128]{3,2,1,0:T(8,128)(2,1)} %bitcast.13, bf16[32,8,8,128]{3,2,1,0:T(8,128)(2,1)} %bitcast.14, bf16[32,8,8,128]{3,2,1,0:T(8,128)(2,1)} %bitcast.15, bf16[32,8,8,128]{3,2,1,0:T(8,128)(2,1)} %bitcast.16, ...), custom_call_target="tpu_custom_call" | custom-call | tf_op jit(solution)/shard_map/section_backward/pallas_call | solution.py:395
  52.5 2.7 %section_finish.1 = (bf16[32,8,8,128]{3,2,1,0:T(8,128)(2,1)}, f32[3,3,3,32,32]{4,3,2,1,0:T(8,128)}, f32[3,3,3,32,32]{4,3,2,1,0:T(8,128)}, f32[1,32]{1,0:T(1,128)...) custom-call(bf16[8,256,128]{2,1,0:T(8,128)(2,1)} %get-tuple-element.17.rows_in, ...), custom_call_target="tpu_custom_call" | custom-call | tf_op jit(solution)/shard_map/section_finish/pallas_call | solution.py:425

commit v3 on v2

--- a/solution.py
+++ b/solution.py
@@ -17,13 +17,13 @@
 
 def body(sizes, cells, c1, c2, ug, vol, w1, w2, g1, b1, g2, b2,
          out, og, small,
-         n1, n2, sl, d1, act, volp, grad, facc, ar, rb, wt, hx, hc, hs,
+         n1, n2, sl, d1, act, volp, grad, facc, fb, ar, rb, wt, hx, hc, hs,
          ar_send, ar_recv, h_send, h_recv, rs_send, rs_recv, ag_send, ag_recv):
     n_dp, n_sx, n_sy = sizes
     n = n_dp * n_sx * n_sy
     ch, nx, ny, nz = c1.shape
     rows = ny * ch
-    tiles = facc.shape[1]
+    tiles = fb.shape[1]
     per = rb.shape[2]
     owners = tiles // per
     i_dp, i_sx, i_sy = [lax.axis_index(a) for a in AXES]
@@ -169,46 +169,58 @@
     def project(k, x):
         w = wt[k, :, pl.ds(0, 27 * ch)]
         pieces = []
-        for y in range(ny):
-            g = jnp.concatenate(
-                [grad[k, x + a, y : y + 3].reshape(9 * ch, nz) for a in range(3)], axis=0)
-            pieces.append(jnp.dot(w, g, preferred_element_type=F32))
+        pair = 2 if ny % 2 == 0 else 1
+        for first in range(0, ny, pair):
+            g = jnp.concatenate([
+                jnp.concatenate(
+                    [grad[k, x + a, y : y + 3].reshape(9 * ch, nz) for a in range(3)], axis=0)
+                for y in range(first, first + pair)], axis=1)
+            r = jnp.dot(w, g, preferred_element_type=F32)
+            pieces += [r[:, i * nz : (i + 1) * nz] for i in range(pair)]
         return jnp.concatenate(pieces, axis=0)
 
     def filters(k, u):
         facc[k] = jnp.zeros(facc.shape[1:], F32)
-
-        @pl.loop(0, nx + 2)
-        def _(x):
+        pair = 2 if nx % 2 == 0 else 1
+
+        @pl.loop(0, (nx + 2) // pair)
+        def _(step):
+            xs = [step * pair + i for i in range(pair)]
             lhs = jnp.concatenate(
-                [grad[k, x, y : y + 3].reshape(9 * ch, nz) for y in range(ny)], axis=1)
+                [grad[k, x, y : y + 3].reshape(9 * ch, nz) for x in xs for y in range(ny)], axis=1)
             rhs = jnp.concatenate(
-                [u[y, pl.ds(x, 3)].reshape(3 * ch, nz) for y in range(ny)], axis=1)
-            rhs = jnp.concatenate([rhs, jnp.zeros((128 - 3 * ch, ny * nz), BF16)], axis=0)
-            r = lax.dot_general(lhs, rhs, NT, preferred_element_type=F32)
-            facc[k] += r.reshape(facc.shape[1:])
+                [u[y, pl.ds(x, 3)].reshape(3 * ch, nz) for x in xs for y in range(ny)], axis=1)
+            rhs = jnp.concatenate(
+                [rhs, jnp.zeros((128 - 3 * ch, rhs.shape[1]), BF16)], axis=0)
+            facc[k] += lax.dot_general(lhs, rhs, NT, preferred_element_type=F32)
+
+        fb[k] = facc[k].reshape(fb.shape[1:]).astype(BF16)
+
+    def place(k, j):
+        return j if k == 0 else n - 1 - j
 
     def start_scatter(k):
         @each_peer
         def _(peer):
             j = (peer[0] * n_sx + peer[1]) * n_sy + peer[2]
 
-            @pl.when(j < owners)
+            @pl.when(place(k, j) < owners)
             def _():
                 pltpu.make_async_remote_copy(
-                    facc.at[k, pl.ds(j * per, per)], rb.at[k, me], rs_send.at[k], rs_recv.at[k],
+                    fb.at[k, pl.ds(place(k, j) * per, per)], rb.at[k, me], rs_send.at[k], rs_recv.at[k],
                     device_id=peer, device_id_type=pl.DeviceIdType.MESH).start()
 
     def wait_bytes(ref, sem):
         pltpu.make_async_copy(ref, ref, sem).wait()
 
     def start_gather(k):
-        @pl.when(me < owners)
+        @pl.when(place(k, me) < owners)
         def _():
-            mine = pl.ds(me * per, per)
-            rb[k, me] = facc[k, mine]
+            mine = pl.ds(place(k, me) * per, per)
+            rb[k, me] = fb[k, mine]
             wait_bytes(rb.at[k, pl.ds(0, n - 1)], rs_recv.at[k])
-            og[k, mine] = jnp.sum(rb[k], axis=0) * (1.0 / math.sqrt(cells))
+            og[k, mine] = (
+                jnp.sum(rb[k].astype(F32), axis=0) * (1.0 / math.sqrt(cells))).astype(BF16)
 
             @each_peer
             def _(peer):
@@ -217,15 +229,15 @@
                     device_id=peer, device_id_type=pl.DeviceIdType.MESH).start()
 
     def end_gather(k):
-        @pl.when(me < owners)
+        @pl.when(place(k, me) < owners)
         def _():
-            wait_bytes(facc.at[k, pl.ds(0, (owners - 1) * per)], rs_send.at[k])
+            wait_bytes(fb.at[k, pl.ds(0, (owners - 1) * per)], rs_send.at[k])
             wait_bytes(og.at[k, pl.ds(0, (owners - 1) * per)], ag_recv.at[k])
             wait_bytes(rb.at[k, pl.ds(0, n - 1)], ag_send.at[k])
 
-        @pl.when(me >= owners)
+        @pl.when(place(k, me) >= owners)
         def _():
-            wait_bytes(facc.at[k], rs_send.at[k])
+            wait_bytes(fb.at[k], rs_send.at[k])
             wait_bytes(og.at[k], ag_recv.at[k])
 
     zero = jnp.zeros((ch, nz), F32)
@@ -345,9 +357,9 @@
     small[1:2] = row * factor
     end_halo(3)
     make_grad(1, row, n1, gain1 * inv1)
-    start_gather(0)
     filters(1, volp)
     start_scatter(1)
+    start_gather(0)
 
     @pl.loop(0, nx)
     def _(x):
@@ -369,7 +381,7 @@
         out[:, x] = v.reshape(ch, ny, nz).astype(BF16)
     for k, f in enumerate((f2, f1)):
         for b in range(9):
-            t = og[k, pl.ds(b * ch // 8, ch // 8)].reshape(ch, 128).T
+            t = og[k, pl.ds(b * ch // 16, ch // 16)].reshape(ch, 128).astype(F32).T
             for kx in range(3):
                 f[kx, 2 - b // 3, 2 - b % 3] = t[kx * ch : (kx + 1) * ch]
     for r, (b, g) in enumerate(((b2, g2), (b1, g1))):
@@ -383,7 +395,7 @@
     n = math.prod(sizes)
     _, ch, nx, ny, nz = volume.shape
     cells = float(volume.shape[0] * nx * ny * nz * n)
-    tiles = 9 * ch // 8
+    tiles = 9 * ch // 16
     per = -(-tiles // n)
     while tiles % per:
         per += 1
@@ -397,7 +409,7 @@
         name="section_backward",
         out_shape=(
             jax.ShapeDtypeStruct((nx, ny * ch, nz), BF16),
-            jax.ShapeDtypeStruct((2, tiles, 8, 128), F32),
+            jax.ShapeDtypeStruct((2, tiles, 16, 128), BF16),
             jax.ShapeDtypeStruct((8, 128), F32),
         ),
         in_specs=[vmem] * 10,
@@ -405,9 +417,10 @@
         scratch_shapes=[
             big, big, big, big, pad_u, pad_u,
             pltpu.VMEM((2, nx + 2, ny + 2, 3, ch, nz), BF16),
-            pltpu.VMEM((2, tiles, 8, 128), F32),
+            pltpu.VMEM((2, 9 * ch, 128), F32),
+            pltpu.VMEM((2, tiles, 16, 128), BF16),
             pltpu.VMEM((3, n, 1, 128), F32),
-            pltpu.VMEM((2, n, per, 8, 128), F32),
+            pltpu.VMEM((2, n, per, 16, 128), BF16),
             pltpu.VMEM((2, ch, -(-27 * ch // 128) * 128), BF16),
             pltpu.VMEM((4, nx + 2, ny + 2, ch, nz), BF16),
             pltpu.VMEM((2, 4, max(nx, ny) + 2, ch, nz), F32),

time: 55.4 us -> 49.3 us (0.89)
  Pallas kernels: 54.5 us -> 48.5 us
    pallas_call x1, Pallas kernels: 51.9 us -> 45.8 us  [per_device(): pl.pallas_call(functools.partial(body, sizes, cells), name='section_backw...]
where the time goes in v3:
time: 49.3 us; the launch traced here: 49.1 us
  Pallas kernels  48.5 us (98%)
  between operations  0.64 us (1%)
    pallas_call x1, Pallas kernels, per_device(): pl.pallas_call(functools.partial(body, sizes, cells), name='section_backw...  45.8 us
    pallas_call x1, Pallas kernels, per_device(): pl.pallas_call(finish, name='section_finish', out_shape=(jax.ShapeDtypeSt...  2.62 us

profile of v3, /device:TPU:0, one launch (start us, length us, event | category | flops | bytes accessed | tf_op | source)
XLA Modules:
  0.0 49.1 jit_solution(17620146329776607705)
XLA Ops:
  0.6 45.8 %section_backward.1 = (bf16[8,256,128]{2,1,0:T(8,128)(2,1)}, bf16[2,18,16,128]{3,2,1,0:T(8,128)(2,1)}, f32[8,128]{1,0:T(8,128)}) custom-call(bf16[32,8,8,128]{3,2,1,0:T(8,128)(2,1)} %bitcast.13, bf16[32,8,8,128]{3,2,1,0:T(8,128)(2,1)} %bitcast.14, bf16[32,8,8,128]{3,2,1,0:T(8,128)(2,1)} %bitcast.15, bf16[32,8,8,128]{3,2,1,0:T(8,128)(2,1)} %bitcast.16, ...), custom_call_target="tpu_custom_call" | custom-call | tf_op jit(solution)/shard_map/section_backward/pallas_call | solution.py:407
  46.5 2.6 %section_finish.1 = (bf16[32,8,8,128]{3,2,1,0:T(8,128)(2,1)}, f32[3,3,3,32,32]{4,3,2,1,0:T(8,128)}, f32[3,3,3,32,32]{4,3,2,1,0:T(8,128)}, f32[1,32]{1,0:T(1,128)...) custom-call(bf16[8,256,128]{2,1,0:T(8,128)(2,1)} %get-tuple-element.17.rows_in, ...), custom_call_target="tpu_custom_call" | custom-call | tf_op jit(solution)/shard_map/section_finish/pallas_call | solution.py:438

commit v4 on v3

--- a/solution.py
+++ b/solution.py
@@ -252,7 +252,7 @@
         new = (v1, v1 * v1, v2, v2 * v2)
         return tuple(a + per_channel(v) for a, v in zip(acc, new))
 
-    parts = lax.fori_loop(0, nx, moments, (zero,) * 4)
+    parts = lax.fori_loop(0, nx, moments, (zero,) * 4, unroll=True)
     pl.semaphore_wait(barrier, n - 1)
     start_sum(0, parts)
     start_halo(0)
@@ -272,7 +272,7 @@
         for at in (0, nx + 2):
             u[:, pl.ds(at, 2)] = jnp.zeros((ny, 2, ch, nz), BF16)
 
-    @pl.loop(0, nx)
+    @pl.loop(0, nx, unroll=True)
     def _(x):
         volp[:, x + 2] = load(vol, x).astype(BF16).reshape(ny, ch, nz)
 
@@ -346,7 +346,7 @@
         hx[3, x + 1, pl.ds(1, ny)] = slope.astype(BF16).reshape(ny, ch, nz)
         return acc[0] + per_channel(slope), acc[1] + per_channel(slope * n1[x])
 
-    start_sum(2, lax.fori_loop(0, nx, slope_one, (zero, zero)))
+    start_sum(2, lax.fori_loop(0, nx, slope_one, (zero, zero), unroll=True))
     start_halo(3)
     filters(0, act)
     start_scatter(0)
@@ -361,11 +361,18 @@
     start_scatter(1)
     start_gather(0)
 
-    @pl.loop(0, nx)
+    split = nx - nx // 4
+
+    @pl.loop(0, split, unroll=True)
     def _(x):
         out[x] = project(1, x).astype(BF16)
 
     start_gather(1)
+
+    @pl.loop(split, nx, unroll=True)
+    def _(x):
+        out[x] = project(1, x).astype(BF16)
+
     end_gather(0)
     end_gather(1)
 

time: 49.3 us -> 47.9 us (0.972)
  Pallas kernels: 48.5 us -> 47 us
    pallas_call x1, Pallas kernels: 45.8 us -> 44.4 us  [per_device(): pl.pallas_call(functools.partial(body, sizes, cells), name='section_backw...]
where the time goes in v4:
time: 47.9 us; the launch traced here: 47.7 us
  Pallas kernels  47 us (98%)
  between operations  0.64 us (1%)
    pallas_call x1, Pallas kernels, per_device(): pl.pallas_call(functools.partial(body, sizes, cells), name='section_backw...  44.4 us
    pallas_call x1, Pallas kernels, per_device(): pl.pallas_call(finish, name='section_finish', out_shape=(jax.ShapeDtypeSt...  2.62 us

profile of v4, /device:TPU:0, one launch (start us, length us, event | category | flops | bytes accessed | tf_op | source)
XLA Modules:
  0.0 47.7 jit_solution(6561675968002995196)
XLA Ops:
  0.6 44.4 %section_backward.1 = (bf16[8,256,128]{2,1,0:T(8,128)(2,1)}, bf16[2,18,16,128]{3,2,1,0:T(8,128)(2,1)}, f32[8,128]{1,0:T(8,128)}) custom-call(bf16[32,8,8,128]{3,2,1,0:T(8,128)(2,1)} %bitcast.13, bf16[32,8,8,128]{3,2,1,0:T(8,128)(2,1)} %bitcast.14, bf16[32,8,8,128]{3,2,1,0:T(8,128)(2,1)} %bitcast.15, bf16[32,8,8,128]{3,2,1,0:T(8,128)(2,1)} %bitcast.16, ...), custom_call_target="tpu_custom_call" | custom-call | tf_op jit(solution)/shard_map/section_backward/pallas_call | solution.py:414
  45.1 2.6 %section_finish.1 = (bf16[32,8,8,128]{3,2,1,0:T(8,128)(2,1)}, f32[3,3,3,32,32]{4,3,2,1,0:T(8,128)}, f32[3,3,3,32,32]{4,3,2,1,0:T(8,128)}, f32[1,32]{1,0:T(1,128)...) custom-call(bf16[8,256,128]{2,1,0:T(8,128)(2,1)} %get-tuple-element.17.rows_in, ...), custom_call_target="tpu_custom_call" | custom-call | tf_op jit(solution)/shard_map/section_finish/pallas_call | solution.py:445
